TPU v7x, 32 devices: a whole 2x2x4 slice. The times are simulated.
32 devices in a mesh: clip: 2 (over y), seq: 4 (over z), head: 4 (over x, core).
Axes of the slice: x: 2, y: 2, z: 4, core: 2. Of those that a mesh axis runs over, the one named last changes fastest.
Arguments:
- queries: bfloat16 [16, 4, 16, 3072], P(('clip', 'head'), 'seq'), parts along dimension 0, may hold values from -15 to 15
- attn_keys: bfloat16 [16, 4, 16, 3072], P(('clip', 'head'), 'seq'), parts along dimension 0, may hold values from -5 to 5
- attn_values: bfloat16 [16, 4, 16, 3072], P(('clip', 'head'), 'seq'), parts along dimension 0, may hold values from -5 to 5
- residual: bfloat16 [16, 4, 16, 5120], P(('clip', 'head'), 'seq'), parts along dimension 0, may hold values from -6 to 6
- out_weight: bfloat16 [3072, 5120], P('head', 'seq'), may hold values from -0.109375 to 0.109375
- out_gate: float32 [5120], replicated, may hold values from 0.3 to 3
- head_shift: float32 [5120], replicated, may hold values from -3 to 3
- head_scale: float32 [5120], replicated, may hold values from -1.5 to 1.5
- head_weight: bfloat16 [5120, 64], replicated, may hold values from -0.078125 to 0.078125
- head_bias: float32 [64], replicated, may hold values from -3 to 3
- conv_weight: bfloat16 [3, 3, 3, 16, 384], replicated, may hold values from -0.3125 to 0.3125
- conv_bias: float32 [384], replicated, may hold values from -3 to 3
- norm_gain: float32 [384], replicated, may hold values from 0.5 to 2
Outputs:
- hidden: bfloat16 [16, 4, 16, 5120], P(('clip', 'head'), 'seq'), parts along dimension 0
- features: bfloat16 [16, 8, 32, 384], P(('clip', 'head'), 'seq'), parts along dimension 0
There are 2 independent parts, one for each index of `clip`. A program takes and returns all parts, laid end to end along the dimension named above; an argument that names none is the same for every part. Nothing has to cross between parts.
All inputs are finite; a program needn't handle non-finite values.
Results may differ from a plain program's by a relative error of at most 0.013.
Values may be sent and summed in bfloat16 or wider, within the bound.
No kernel may reach another device: no remote copies, remote signals or barrier semaphores. Data moves between devices by JAX's collectives and lax.ppermute only.
A program may use at most 128 MiB of HBM per device.

v0:
```python
import jax
import jax.numpy as jnp
from jax import lax
from jax.sharding import PartitionSpec as P

HEAD_DIM = 128


def from_behind(value, axis, steps):
    count = lax.axis_size(axis)
    first, last = (max(0, -steps), min(count, count - steps))
    return lax.ppermute(value, axis, [(source, source + steps) for source in range(first, last)])


def padded_2(x, sides, width):
    for axis, dim in sides:
        peers, length = (lax.axis_size(axis), x.shape[dim])
        up = [(i, (i + 1) % peers) for i in range(peers - 1)]
        down = [(j, i) for i, j in up]
        last = lax.slice_in_dim(x, length - width, length, axis=dim)
        first = lax.slice_in_dim(x, 0, width, axis=dim)
        before = lax.ppermute(last, axis, up)
        after = lax.ppermute(first, axis, down)
        x = jnp.concatenate([before, x, after], axis=dim)
    return x


def head_latent(hidden, head_shift, head_scale, head_weight, head_bias):
    values = hidden.astype(jnp.float32)
    center = values - jnp.mean(values, -1, keepdims=True)
    spread = jnp.mean(center * center, -1, keepdims=True)
    normed = (center * lax.rsqrt(spread + 1e-06) * (1.0 + head_scale) + head_shift).astype(
        jnp.bfloat16
    )
    flat = normed.reshape(-1, normed.shape[-1])
    latent = (jnp.dot(flat, head_weight, preferred_element_type=jnp.float32) + head_bias).astype(
        jnp.bfloat16
    )
    frames, height, breadth = (hidden.shape[0], hidden.shape[1], hidden.shape[2])
    channels = head_weight.shape[1] // 4
    patches = latent.reshape(frames, height, breadth, 2, 2, channels).transpose(0, 1, 3, 2, 4, 5)
    return patches.reshape(frames, height * 2, breadth * 2, channels)


def convolve(padded, frames, conv_weight, conv_bias, norm_gain):
    height = padded.shape[1] - 2
    breadth = padded.shape[2] - 2
    stacked = jnp.concatenate(
        [
            padded[
                time_off : time_off + frames,
                row_off : row_off + height,
                col_off : col_off + breadth,
            ]
            for time_off in range(3)
            for row_off in range(3)
            for col_off in range(3)
        ],
        -1,
    )
    kernel = conv_weight.reshape(-1, conv_weight.shape[-1])
    linear = (
        jnp.dot(stacked.reshape(-1, stacked.shape[-1]), kernel, preferred_element_type=jnp.float32)
        + conv_bias
    )
    normed = linear * lax.rsqrt(jnp.mean(linear * linear, -1, keepdims=True) + 1e-06) * norm_gain
    return jax.nn.silu(normed).astype(jnp.bfloat16).reshape(frames, height, breadth, -1)


def attend_block(carried, block_keys, block_values, query_heads):
    running, denominator, weighted = carried
    scores = jnp.einsum("hqd,khd->hqk", query_heads, block_keys, preferred_element_type=jnp.float32)
    scores = scores * query_heads.shape[-1] ** (-0.5)
    newmax = jnp.maximum(running, jnp.max(scores, -1))
    factor = jnp.exp(running - newmax)
    weights = jnp.exp(scores - newmax[..., None])
    denominator = denominator * factor + jnp.sum(weights, -1)
    product = jnp.einsum(
        "hqk,khd->hqd",
        weights.astype(jnp.bfloat16),
        block_values,
        preferred_element_type=jnp.float32,
    )
    weighted = weighted * factor[..., None] + product
    return (newmax, denominator, weighted)


def fold_pieces(query_heads, carried, pieces):
    key_piece, value_piece = pieces
    frames, height, breadth = (key_piece.shape[0], key_piece.shape[1], key_piece.shape[2])
    heads_here, head_width = (query_heads.shape[0], query_heads.shape[2])
    group_rows = 4

    def regroup(one_piece):
        shaped = one_piece.reshape(
            frames, height // group_rows, group_rows, breadth, heads_here, head_width
        )
        shaped = shaped.transpose(1, 0, 2, 3, 4, 5)
        return shaped.reshape(
            height // group_rows, frames * group_rows * breadth, heads_here, head_width
        )

    def advance(inner, blocks):
        return (attend_block(inner, blocks[0], blocks[1], query_heads), None)

    carried, _ = lax.scan(advance, carried, (regroup(key_piece), regroup(value_piece)))
    return carried


def on_device(
    queries,
    attn_keys,
    attn_values,
    residual,
    out_weight,
    out_gate,
    head_shift,
    head_scale,
    head_weight,
    head_bias,
    conv_weight,
    conv_bias,
    norm_gain,
):
    head_count = lax.axis_size("head")
    frames_dev = queries.shape[0]
    group_width = queries.shape[3] // head_count
    head_width = HEAD_DIM
    heads_here = group_width // head_width
    local_queries, local_keys, local_values = (
        lax.all_to_all(queries, "head", split_axis=3, concat_axis=0, tiled=True),
        lax.all_to_all(attn_keys, "head", split_axis=3, concat_axis=0, tiled=True),
        lax.all_to_all(attn_values, "head", split_axis=3, concat_axis=0, tiled=True),
    )
    frames_all, height, breadth = (
        local_queries.shape[0],
        local_queries.shape[1],
        local_queries.shape[2],
    )
    count = frames_all * height * breadth
    query_heads = local_queries.reshape(count, heads_here, head_width).transpose(1, 0, 2)
    initial = (
        jnp.full((heads_here, count), -1e30, jnp.float32),
        jnp.zeros((heads_here, count), jnp.float32),
        jnp.zeros((heads_here, count, head_width), jnp.float32),
    )
    carried = fold_pieces(
        query_heads,
        initial,
        (
            lax.all_gather(local_keys, "seq", axis=1, tiled=True),
            lax.all_gather(local_values, "seq", axis=1, tiled=True),
        ),
    )
    running, denominator, weighted = carried
    attended = (weighted / denominator[..., None]).astype(jnp.bfloat16)
    attended = attended.transpose(1, 0, 2).reshape(count, group_width)
    partial_value = jnp.dot(
        attended,
        lax.all_gather(out_weight, "seq", axis=1, tiled=True),
        preferred_element_type=jnp.float32,
    )
    partial_value = partial_value.reshape(frames_all, height, breadth, partial_value.shape[-1])
    owned = lax.psum_scatter(
        partial_value.astype(jnp.bfloat16), "head", scatter_dimension=0, tiled=True
    ).astype(jnp.float32)
    hidden = (residual.astype(jnp.float32) + out_gate * owned).astype(jnp.bfloat16)
    own_video = head_latent(hidden, head_shift, head_scale, head_weight, head_bias)
    earlier = from_behind(own_video, "head", 1)
    video = jnp.concatenate([earlier, own_video], 0)
    extended = padded_2(video, (("seq", 1),), 1)
    padded = jnp.pad(extended, ((0, 0), (0, 0), (1, 1), (0, 0)))
    features = convolve(padded, frames_dev, conv_weight, conv_bias, norm_gain)
    return (hidden, features)


def solution(mesh):
    return jax.shard_map(
        on_device,
        mesh=mesh,
        in_specs=(
            P(("clip", "head"), "seq", None, None),
            P(("clip", "head"), "seq", None, None),
            P(("clip", "head"), "seq", None, None),
            P(("clip", "head"), "seq", None, None),
            P("head", "seq"),
            P(),
            P(),
            P(),
            P(),
            P(),
            P(),
            P(),
            P(),
        ),
        out_specs=(P(("clip", "head"), "seq", None, None), P(("clip", "head"), "seq", None, None)),
        check_vma=False,
    )
```

profile of v0, /device:TPU:2, one launch (start us, length us, event | category | flops | bytes accessed | tf_op | source)
XLA Modules:
  0.0 232.1 jit_solution(3632974338613475676)
XLA Ops:
  7.2 0.7 all-gather.2.cloned.1.call-update
  7.9 0.2 copy-done.5
  8.2 1.8 copy.79
  10.0 2.3 reshape.122
  12.3 3.4 %all-to-all-start.1 = ((bf16[4,2,12288]{2,1,0:T(2,128)(2,1)}), bf16[4,2,12288]{2,1,0:T(2,128)(2,1)S(1)}, u32[]{:S(2)}, u32[]{:S(2)}) async-start(bf16[4,2,12288]{2,1,0:T(2,128)(2,1)} %reshape.122), calls=%async_computation.1 | async-start | bytes 393216 | tf_op jit(solution)/shard_map/all_to_all | solution.py:132
  15.6 1.8 copy.75
  17.5 2.3 reshape.124
  19.8 4.4 %all-to-all-start = ((bf16[4,2,12288]{2,1,0:T(2,128)(2,1)}), bf16[4,2,12288]{2,1,0:T(2,128)(2,1)S(1)}, u32[]{:S(2)}, u32[]{:S(2)}) async-start(bf16[4,2,12288]{2,1,0:T(2,128)(2,1)} %reshape.124), calls=%async_computation | async-start | bytes 393216 | tf_op jit(solution)/shard_map/all_to_all | solution.py:131
  24.2 1.8 copy.84
  26.0 2.3 reshape.126
  28.3 1.2 reshape.123
  29.4 1.1 copy.93
  30.6 4.0 %all-to-all-start.2 = ((bf16[4,2,12288]{2,1,0:T(2,128)(2,1)}), bf16[4,2,12288]{2,1,0:T(2,128)(2,1)}, u32[]{:S(2)}, u32[]{:S(2)}) async-start(bf16[4,2,12288]{2,1,0:T(2,128)(2,1)} %reshape.126), calls=%async_computation.2 | async-start | bytes 393216 | tf_op jit(solution)/shard_map/all_to_all | solution.py:133
  34.7 35.2 %all_gather.9 = bf16[8,4,16,768]{3,2,0,1:T(8,128)(2,1)S(1)} all-gather(bf16[8,1,16,768]{3,2,0,1:T(8,128)(2,1)S(1)} %bitcast.111), channel_id=1, replica_groups=mesh['clip'=2,'seq'=4,'head'=4] {'seq'}, dimensions={1}, use_global_device_ids=true | all-gather | bytes 983040 | tf_op jit(solution)/shard_map/all_gather | solution.py:151
  70.0 0.9 squeeze.9
  70.8 1.2 reshape.125
  72.0 1.1 copy.92
  73.1 0.2 reshape.115
  73.4 5.6 %reshape.127 = bf16[3072,1,2,16]{3,2,1,0:T(2,128)(2,1)S(1)} reshape(bf16[4,2,12288]{2,1,0:T(2,128)(2,1)} %all-to-all-done.2) | data formatting | bytes 393216
  79.0 2.5 %copy.94 = bf16[2,1,16,4,768]{4,3,2,0,1:T(4,128)(2,1)} copy(bf16[2,1,16,4,768]{2,0,4,3,1:T(2,128)(2,1)S(1)} %bitcast.95) | data formatting | bytes 393216 | tf_op jit(solution)/shard_map/all_to_all | solution.py:133
  81.5 1.0 copy.86
  82.4 32.4 %all_gather.10 = bf16[8,4,16,768]{3,2,0,1:T(8,128)(2,1)S(1)} all-gather(bf16[8,1,16,768]{3,2,0,1:T(8,128)(2,1)S(1)} %bitcast.112), channel_id=1, replica_groups=mesh['clip'=2,'seq'=4,'head'=4] {'seq'}, dimensions={1}, use_global_device_ids=true | all-gather | bytes 983040 | tf_op jit(solution)/shard_map/all_gather | solution.py:152
  114.9 1.9 squeeze.10
  116.8 0.5 fusion.35
  117.3 0.5 fusion.8
  117.8 0.2 copy-done.2
  118.0 0.6 fusion.12
  118.7 0.1 copy.89
  118.8 0.2 dot_general.24
  119.1 57.9 %all-gather.2.cloned.1.call-done = bf16[768,5120]{1,0:T(8,128)(2,1)} async-done(((bf16[768,1280]{1,0:T(8,128)(2,1)}), bf16[768,5120]{1,0:T(8,128)(2,1)}) %all-gather.2.cloned.1.call-update) | async-done | bytes 7864336 | tf_op jit(solution)/shard_map/all_gather | solution.py:160
  177.0 5.6 %fusion.5 = bf16[8,1,16,5120]{3,2,0,1:T(8,128)(2,1)} fusion(bf16[8,16,768]{2,1,0:T(8,128)(2,1)S(1)} %dot_general.24, bf16[768,5120]{1,0:T(8,128)(2,1)} %all-gather.2.cloned.1.call-done), kind=kOutput, calls=%fused_computation.3 | convolution fusion | flops 1007288320 | bytes 9371648 | tf_op jit(solution)/shard_map/dot_general | solution.py:158
  182.6 23.7 %reduce-scatter.2.cloned.1.call-done = bf16[2,1,16,5120]{3,2,0,1:T(8,128)(2,1)} async-done(((bf16[8,1,16,5120]{3,2,0,1:T(8,128)(2,1)}), bf16[2,1,16,5120]{3,2,0,1:T(8,128)(2,1)}) %reduce-scatter.2.cloned.1.call-update) | async-done | bytes 327696 | tf_op jit(solution)/shard_map/reduce_scatter | solution.py:164
  206.3 1.2 convert_reduce_fusion
  207.5 0.2 fusion.20
  207.8 0.2 fusion.23
  208.0 0.3 fusion.13
  208.3 0.1 reshape.117
  208.4 1.9 collective-permute-start
  210.4 3.3 %collective-permute-done = bf16[2,2,32,16]{3,2,1,0:T(8,128)(2,1)S(1)} collective-permute-done((bf16[2,2,32,16]{3,2,1,0:T(8,128)(2,1)S(1)}, bf16[2,2,32,16]{3,2,1,0:T(8,128)(2,1)S(1)}, u32[]{:S(2)}, u32[]{:S(2)}) %collective-permute-start) | collective-permute-done | bytes 4128 | tf_op jit(solution)/shard_map/ppermute | solution.py:12
  213.7 3.6 %collective-permute-start.1 = (bf16[4,1,32,16]{3,2,1,0:T(8,128)(2,1)S(1)}, bf16[4,1,32,16]{3,2,1,0:T(8,128)(2,1)S(1)}, u32[]{:S(2)}, u32[]{:S(2)}) collective-permute-start(bf16[4,1,32,16]{3,2,1,0:T(8,128)(2,1)S(1)} %get-tuple-element.63), channel_id=1, source_target_pairs={{0,4},{4,8},{8,12},{1,5},{5,9},{9,13},{2,6},{6,10},{10,14},{3,7},{... | collective-permute-start | bytes 12296 | tf_op jit(solution)/shard_map/ppermute | solution.py:22
  217.3 1.3 collective-permute-start.2
  218.6 0.3 collective-permute-done.1
  218.9 4.2 %collective-permute-done.2 = bf16[4,1,32,16]{3,2,1,0:T(8,128)(2,1)S(1)} collective-permute-done((bf16[4,1,32,16]{3,2,1,0:T(8,128)(2,1)S(1)}, bf16[4,1,32,16]{3,2,1,0:T(8,128)(2,1)S(1)}, u32[]{:S(2)}, u32[]{:S(2)}) %collective-permute-start.2) | collective-permute-done | bytes 4128 | tf_op jit(solution)/shard_map/ppermute | solution.py:23
  223.2 0.1 fusion.32
  223.4 0.3 concatenate.105
  223.7 0.4 copy-done.3
  224.2 0.3 multiply_reduce_fusion
  224.5 0.8 multiply_convert_fusion
  (47 shorter events, 0.6 us)
Async XLA Ops:
  7.2 200.8 %copy-start = (bf16[5120,64]{0,1:T(8,128)(2,1)S(1)}, bf16[5120,64]{0,1:T(8,128)(2,1)}, u32[]{:S(2)}) copy-start(bf16[5120,64]{0,1:T(8,128)(2,1)} %param.21) | copy-start | bytes 1966084
  7.2 1.0 copy-start.5
  7.2 169.8 %all-gather.2.cloned.1.call-start = ((), (), s32[]{:S(2)}) async-start(), calls=%async_computation.4 | async-start | bytes 9830400 | tf_op jit(solution)/shard_map/all_gather | solution.py:160
  8.2 7.4 %copy-start.6 = (bf16[2,1,16,3072]{3,2,1,0:T(8,128)(2,1)S(1)}, bf16[2,1,16,3072]{3,2,1,0:T(8,128)(2,1)}, u32[]{:S(2)}) copy-start(bf16[2,1,16,3072]{3,2,1,0:T(8,128)(2,1)} %param.13) | copy-start | bytes 589828
  12.3 7.5 %all-to-all-start.1 = ((bf16[4,2,12288]{2,1,0:T(2,128)(2,1)}), bf16[4,2,12288]{2,1,0:T(2,128)(2,1)S(1)}, u32[]{:S(2)}, u32[]{:S(2)}) async-start(bf16[4,2,12288]{2,1,0:T(2,128)(2,1)} %reshape.122), calls=%async_computation.1 | async-start | bytes 393216 | tf_op jit(solution)/shard_map/all_to_all | solution.py:132
  17.5 6.7 %copy-start.7 = (bf16[2,1,16,3072]{3,2,1,0:T(8,128)(2,1)S(1)}, bf16[2,1,16,3072]{3,2,1,0:T(8,128)(2,1)}, u32[]{:S(2)}) copy-start(bf16[2,1,16,3072]{3,2,1,0:T(8,128)(2,1)} %param.15) | copy-start | bytes 589828
  19.8 10.8 %all-to-all-start = ((bf16[4,2,12288]{2,1,0:T(2,128)(2,1)}), bf16[4,2,12288]{2,1,0:T(2,128)(2,1)S(1)}, u32[]{:S(2)}, u32[]{:S(2)}) async-start(bf16[4,2,12288]{2,1,0:T(2,128)(2,1)} %reshape.124), calls=%async_computation | async-start | bytes 393216 | tf_op jit(solution)/shard_map/all_to_all | solution.py:131
  30.6 42.8 %all-to-all-start.2 = ((bf16[4,2,12288]{2,1,0:T(2,128)(2,1)}), bf16[4,2,12288]{2,1,0:T(2,128)(2,1)}, u32[]{:S(2)}, u32[]{:S(2)}) async-start(bf16[4,2,12288]{2,1,0:T(2,128)(2,1)} %reshape.126), calls=%async_computation.2 | async-start | bytes 393216 | tf_op jit(solution)/shard_map/all_to_all | solution.py:133
  34.6 171.7 %reduce-scatter.2.cloned.1.call-start = ((), (), s32[]{:S(2)}) async-start(), calls=%async_computation.5 | async-start | bytes 1638400 | tf_op jit(solution)/shard_map/reduce_scatter | solution.py:164
  116.8 1.2 copy-start.2
  119.1 63.5 %copy-start.9 = (f32[5120]{0:T(1024)S(1)}, f32[5120]{0:T(1024)}, u32[]{:S(2)}) copy-start(f32[5120]{0:T(1024)} %param.20) | copy-start | bytes 61444
  119.1 87.2 %copy-start.10 = (f32[5120]{0:T(1024)S(1)}, f32[5120]{0:T(1024)}, u32[]{:S(2)}) copy-start(f32[5120]{0:T(1024)} %param.18) | copy-start | bytes 61444
  182.6 23.8 %copy-start.4 = (bf16[2,1,16,5120]{3,2,1,0:T(8,128)(2,1)S(1)}, bf16[2,1,16,5120]{3,2,1,0:T(8,128)(2,1)}, u32[]{:S(2)}) copy-start(bf16[2,1,16,5120]{3,2,1,0:T(8,128)(2,1)} %param.16) | copy-start | bytes 983044
  182.6 25.2 %copy-start.8 = (f32[5120]{0:T(1024)S(1)}, f32[5120]{0:T(1024)}, u32[]{:S(2)}) copy-start(f32[5120]{0:T(1024)} %param.19) | copy-start | bytes 61444
  182.6 25.4 %copy-start.13 = (f32[64]{0:T(128)S(1)}, f32[64]{0:T(128)}, u32[]{:S(2)}) copy-start(f32[64]{0:T(128)} %param.22) | copy-start | bytes 772
  207.5 15.8 %copy-start.1 = (bf16[2,1,16,5120]{3,2,0,1:T(8,128)(2,1)}, bf16[2,1,16,5120]{3,2,0,1:T(8,128)(2,1)S(1)}, u32[]{:S(2)}) copy-start(bf16[2,1,16,5120]{3,2,0,1:T(8,128)(2,1)S(1)} %get-tuple-element.36) | copy-start | bytes 983044
  208.4 5.2 %collective-permute-start = (bf16[2,2,32,16]{3,2,1,0:T(8,128)(2,1)S(1)}, bf16[2,2,32,16]{3,2,1,0:T(8,128)(2,1)S(1)}, u32[]{:S(2)}, u32[]{:S(2)}) collective-permute-start(bf16[2,2,32,16]{3,2,1,0:T(8,128)(2,1)S(1)} %bitcast.101), channel_id=1, source_target_pairs={{0,1},{1,2},{2,3},{4,5},{5,6},{6,7},{8,9},{9,10},{10,11},{12,13},{... | collective-permute-start | bytes 12296 | tf_op jit(solution)/shard_map/ppermute | solution.py:12
  213.7 5.2 %collective-permute-start.1 = (bf16[4,1,32,16]{3,2,1,0:T(8,128)(2,1)S(1)}, bf16[4,1,32,16]{3,2,1,0:T(8,128)(2,1)S(1)}, u32[]{:S(2)}, u32[]{:S(2)}) collective-permute-start(bf16[4,1,32,16]{3,2,1,0:T(8,128)(2,1)S(1)} %get-tuple-element.63), channel_id=1, source_target_pairs={{0,4},{4,8},{8,12},{1,5},{5,9},{9,13},{2,6},{6,10},{10,14},{3,7},{... | collective-permute-start | bytes 12296 | tf_op jit(solution)/shard_map/ppermute | solution.py:22
  217.3 5.8 %collective-permute-start.2 = (bf16[4,1,32,16]{3,2,1,0:T(8,128)(2,1)S(1)}, bf16[4,1,32,16]{3,2,1,0:T(8,128)(2,1)S(1)}, u32[]{:S(2)}, u32[]{:S(2)}) collective-permute-start(bf16[4,1,32,16]{3,2,1,0:T(8,128)(2,1)S(1)} %get-tuple-element.64), channel_id=1, source_target_pairs={{4,0},{8,4},{12,8},{5,1},{9,5},{13,9},{6,2},{10,6},{14,10},{7,3},{... | collective-permute-start | bytes 12296 | tf_op jit(solution)/shard_map/ppermute | solution.py:23
  223.2 1.0 copy-start.3
  223.2 1.0 copy-start.11
  223.2 1.3 copy-start.12
Sparse Core Ops, SparseCore 0:
  9.6 167.3 all-gather.1
  182.7 23.5 reduce-scatter.1
where the time goes:
time: 233 us; the launch traced here: 232 us
  waiting for transfers between devices  90.1 us (39%)
  blocking collectives  67.6 us (29%)
  local copies, waits for them, and re-layouts  30.9 us (13%)
  starting transfers between devices  18.7 us (8%)
  between operations  14.4 us (6%)
  matrix products  7.28 us (3%)
  other arithmetic  3.08 us (1%)
    all_gather x1, waiting for transfers between devices, on_device(): lax.all_gather(out_weight, 'seq', axis=1, tiled=True)  57.9 us
    all_gather x1, blocking collectives, on_device(): lax.all_gather(local_keys, 'seq', axis=1, tiled=True)  35.2 us
    all_gather x1, blocking collectives, on_device(): lax.all_gather(local_values, 'seq', axis=1, tiled=True)  32.4 us
    reduce_scatter x1, waiting for transfers between devices, on_device(): lax.psum_scatter(partial_value.astype(jnp.bfloat16), 'head', scatter_dime...  23.7 us
    unnamed x37, local copies, waits for them, and re-layouts  21.1 us
    dot_general x1, matrix products, on_device(): jnp.dot(attended, lax.all_gather(out_weight, 'seq', axis=1, tiled=True),...  5.58 us
  transfers between devices with their start and end apart: 8, of which 5 were waited for; matrix products, arithmetic and copies ran while one was open for 13% of the time, Pallas kernels for 0%

commit v1 on v0

--- a/solution.py
+++ b/solution.py
@@ -122,6 +122,26 @@
     conv_bias,
     norm_gain,
 ):
+
+    def pack_sizes(array_axis, u_in):
+        dev_axis = "seq"
+        many = lax.axis_size(dev_axis)
+        all_blocks = [u_in]
+        for t in range(1, many):
+            all_blocks.append(
+                lax.ppermute(
+                    all_blocks[t - 1],
+                    axis_name=dev_axis,
+                    perm=[(dev_i, (dev_i - 1) % many) for dev_i in range(many)],
+                )
+            )
+        answer = jnp.roll(
+            jnp.concatenate(all_blocks, array_axis),
+            lax.axis_index(dev_axis) * u_in.shape[array_axis],
+            array_axis,
+        )
+        return answer
+
     head_count = lax.axis_size("head")
     frames_dev = queries.shape[0]
     group_width = queries.shape[3] // head_count
@@ -147,10 +167,7 @@
     carried = fold_pieces(
         query_heads,
         initial,
-        (
-            lax.all_gather(local_keys, "seq", axis=1, tiled=True),
-            lax.all_gather(local_values, "seq", axis=1, tiled=True),
-        ),
+        (pack_sizes(1, local_keys), lax.all_gather(local_values, "seq", axis=1, tiled=True)),
     )
     running, denominator, weighted = carried
     attended = (weighted / denominator[..., None]).astype(jnp.bfloat16)

time: 233 us -> 233 us (level)
  waiting for transfers between devices: 90.1 us -> 108 us
  blocking collectives: 67.6 us -> 51.1 us
  local copies, waits for them, and re-layouts: 30.9 us -> 27.7 us
    all_gather x1 -> x0, blocking collectives: 35.2 us -> none  [on_device(): lax.all_gather(local_keys, 'seq', axis=1, tiled=True)]
    ppermute x0 -> x3, waiting for transfers between devices: none -> 13.6 us  [pack_sizes(): lax.ppermute(all_blocks[t - 1], axis_name=dev_axis, perm=[(dev_i, (dev_i...]
    all_gather x1, blocking collectives: 32.4 us -> 44.4 us  [on_device(): lax.all_gather(local_values, 'seq', axis=1, tiled=True)]
    all_to_all x0 -> x1, blocking collectives: none -> 6.76 us  [on_device(): lax.all_to_all(attn_keys, 'head', split_axis=3, concat_axis=0, tiled=True)]
    ppermute x0 -> x3, starting transfers between devices: none -> 4.39 us  [pack_sizes(): lax.ppermute(all_blocks[t - 1], axis_name=dev_axis, perm=[(dev_i, (dev_i...]
    all_gather x1, waiting for transfers between devices: 57.9 us -> 61.4 us  [on_device(): lax.all_gather(out_weight, 'seq', axis=1, tiled=True)]
    all_to_all x1 -> x0, starting transfers between devices: 3.36 us -> none  [on_device(): lax.all_to_all(attn_keys, 'head', split_axis=3, concat_axis=0, tiled=True)]
    all_to_all x2, local copies, waits for them, and re-layouts: 3.47 us -> 1.11 us  [on_device(): lax.all_to_all(attn_values, 'head', split_axis=3, concat_axis=0, tiled=True)]
  transfers between devices with their start and end apart: 8 -> 10, of which waited for: 5 -> 6; matrix products, arithmetic and copies ran while one was open for 13% -> 12% of each run, Pallas kernels for 0% -> 0%
where the time goes in v1:
time: 233 us; the launch traced here: 232 us
  waiting for transfers between devices  108 us (46%)
  blocking collectives  51.1 us (22%)
  local copies, waits for them, and re-layouts  27.7 us (12%)
  starting transfers between devices  20.7 us (9%)
  between operations  14.5 us (6%)
  matrix products  7.22 us (3%)
  other arithmetic  2.78 us (1%)
    all_gather x1, waiting for transfers between devices, on_device(): lax.all_gather(out_weight, 'seq', axis=1, tiled=True)  61.4 us
    all_gather x1, blocking collectives, on_device(): lax.all_gather(local_values, 'seq', axis=1, tiled=True)  44.4 us
    reduce_scatter x1, waiting for transfers between devices, on_device(): lax.psum_scatter(partial_value.astype(jnp.bfloat16), 'head', scatter_dime...  24.5 us
    unnamed x44, local copies, waits for them, and re-layouts  20.2 us
    ppermute x3, waiting for transfers between devices, pack_sizes(): lax.ppermute(all_blocks[t - 1], axis_name=dev_axis, perm=[(dev_i, (dev_i...  13.6 us
    all_to_all x1, blocking collectives, on_device(): lax.all_to_all(attn_keys, 'head', split_axis=3, concat_axis=0, tiled=True)  6.76 us
    dot_general x1, matrix products, on_device(): jnp.dot(attended, lax.all_gather(out_weight, 'seq', axis=1, tiled=True),...  5.58 us
    all_to_all x1, starting transfers between devices, on_device(): lax.all_to_all(attn_values, 'head', split_axis=3, concat_axis=0, tiled=True)  4.97 us
  transfers between devices with their start and end apart: 10, of which 6 were waited for; matrix products, arithmetic and copies ran while one was open for 12% of the time, Pallas kernels for 0%

profile of v1, /device:TPU:2, one launch (start us, length us, event | category | flops | bytes accessed | tf_op | source)
XLA Modules:
  0.0 232.0 jit_solution(13914991369603621615)
XLA Ops:
  7.2 0.7 all-gather.2.cloned.1.call-update
  7.9 0.2 copy-done.5
  8.2 1.8 copy.80
  10.0 1.6 reshape.122
  11.6 6.8 %all_to_all.51 = bf16[4,2,12288]{2,1,0:T(2,128)(2,1)S(1)} all-to-all(bf16[4,2,12288]{2,1,0:T(2,128)(2,1)S(1)} %reshape.122), channel_id=1, replica_groups=mesh['clip'=2,'seq'=4,'head'=4] {'head'}, dimensions={0} | all-to-all | bytes 393216 | tf_op jit(solution)/shard_map/all_to_all | solution.py:152
  18.3 1.2 reshape.123
  19.5 1.1 copy.99
  20.6 3.7 %collective-permute-start = (bf16[8,1,16,768]{3,2,0,1:T(8,128)(2,1)S(1)}, bf16[8,1,16,768]{3,2,0,1:T(8,128)(2,1)}, u32[]{:S(2)}, u32[]{:S(2)}) collective-permute-start(bf16[8,1,16,768]{3,2,0,1:T(8,128)(2,1)S(1)} %bitcast.110), channel_id=1, source_target_pairs={{0,12},{4,0},{8,4},{12,8},{1,13},{5,1},{9,5},{13,9},{2,14},{6,2},{... | collective-permute-start | bytes 589832 | tf_op jit(solution)/shard_map/ppermute | solution.py:132
  24.3 1.8 copy.89
  26.1 2.3 reshape.126
  28.4 5.0 %all-to-all-start.2 = ((bf16[4,2,12288]{2,1,0:T(2,128)(2,1)}), bf16[4,2,12288]{2,1,0:T(2,128)(2,1)S(1)}, u32[]{:S(2)}, u32[]{:S(2)}) async-start(bf16[4,2,12288]{2,1,0:T(2,128)(2,1)} %reshape.126), calls=%async_computation.2 | async-start | bytes 393216 | tf_op jit(solution)/shard_map/all_to_all | solution.py:153
  33.4 1.8 copy.84
  35.2 2.3 reshape.124
  37.5 4.6 %all-to-all-start.1 = ((bf16[4,2,12288]{2,1,0:T(2,128)(2,1)}), bf16[4,2,12288]{2,1,0:T(2,128)(2,1)S(1)}, u32[]{:S(2)}, u32[]{:S(2)}) async-start(bf16[4,2,12288]{2,1,0:T(2,128)(2,1)} %reshape.124), calls=%async_computation.1 | async-start | bytes 393216 | tf_op jit(solution)/shard_map/all_to_all | solution.py:151
  42.0 1.2 reshape.127
  43.2 1.1 copy.101
  44.3 0.5 collective-permute-start.1
  44.8 44.4 %all_gather.6 = bf16[8,4,16,768]{3,2,0,1:T(8,128)(2,1)S(1)} all-gather(bf16[8,1,16,768]{3,2,0,1:T(8,128)(2,1)S(1)} %bitcast.124), channel_id=1, replica_groups=mesh['clip'=2,'seq'=4,'head'=4] {'seq'}, dimensions={1}, use_global_device_ids=true | all-gather | bytes 983040 | tf_op jit(solution)/shard_map/all_gather | solution.py:170
  89.2 1.2 reshape.125
  90.4 1.1 copy.100
  91.5 0.2 reshape.115
  91.8 1.9 squeeze.10
  93.8 0.2 collective-permute-start.2
  94.0 0.9 constant_dynamic-update-slice_fusion.6
  94.9 0.9 constant_dynamic-update-slice_fusion.5
  95.9 13.6 %collective-permute-done.2 = bf16[8,1,16,768]{3,2,0,1:T(8,128)(2,1)S(1)} collective-permute-done((bf16[8,1,16,768]{3,2,0,1:T(8,128)(2,1)}, bf16[8,1,16,768]{3,2,0,1:T(8,128)(2,1)S(1)}, u32[]{:S(2)}, u32[]{:S(2)}) %collective-permute-start.2) | collective-permute-done | bytes 196640 | tf_op jit(solution)/shard_map/ppermute | solution.py:132
  109.5 0.9 constant_dynamic-update-slice_fusion.2
  110.4 0.9 constant_dynamic-update-slice_fusion.1
  111.6 0.9 squeeze.9
  112.5 0.4 bitcast_reduce_fusion
  113.1 0.6 copy-done.2
  113.7 0.7 fusion.13
  114.5 0.2 dot_general.24
  114.8 61.4 %all-gather.2.cloned.1.call-done = bf16[768,5120]{1,0:T(8,128)(2,1)} async-done(((bf16[768,1280]{1,0:T(8,128)(2,1)}), bf16[768,5120]{1,0:T(8,128)(2,1)}) %all-gather.2.cloned.1.call-update) | async-done | bytes 7864336 | tf_op jit(solution)/shard_map/all_gather | solution.py:177
  176.2 5.6 %fusion.5 = bf16[8,1,16,5120]{3,2,0,1:T(8,128)(2,1)} fusion(bf16[8,16,768]{2,1,0:T(8,128)(2,1)S(1)} %dot_general.24, bf16[768,5120]{1,0:T(8,128)(2,1)} %all-gather.2.cloned.1.call-done), kind=kOutput, calls=%fused_computation.3 | convolution fusion | flops 1007288320 | bytes 9371648 | tf_op jit(solution)/shard_map/dot_general | solution.py:175
  181.8 24.5 %reduce-scatter.2.cloned.1.call-done = bf16[2,1,16,5120]{3,2,0,1:T(8,128)(2,1)} async-done(((bf16[8,1,16,5120]{3,2,0,1:T(8,128)(2,1)}), bf16[2,1,16,5120]{3,2,0,1:T(8,128)(2,1)}) %reduce-scatter.2.cloned.1.call-update) | async-done | bytes 327696 | tf_op jit(solution)/shard_map/reduce_scatter | solution.py:181
  206.3 1.2 convert_reduce_fusion
  208.0 0.3 fusion.14
  208.4 1.9 collective-permute-start.3
  210.3 3.3 %collective-permute-done.3 = bf16[2,2,32,16]{3,2,1,0:T(8,128)(2,1)S(1)} collective-permute-done((bf16[2,2,32,16]{3,2,1,0:T(8,128)(2,1)S(1)}, bf16[2,2,32,16]{3,2,1,0:T(8,128)(2,1)S(1)}, u32[]{:S(2)}, u32[]{:S(2)}) %collective-permute-start.3) | collective-permute-done | bytes 4128 | tf_op jit(solution)/shard_map/ppermute | solution.py:12
  213.6 3.6 %collective-permute-start.4 = (bf16[4,1,32,16]{3,2,1,0:T(8,128)(2,1)S(1)}, bf16[4,1,32,16]{3,2,1,0:T(8,128)(2,1)S(1)}, u32[]{:S(2)}, u32[]{:S(2)}) collective-permute-start(bf16[4,1,32,16]{3,2,1,0:T(8,128)(2,1)S(1)} %get-tuple-element.63), channel_id=1, source_target_pairs={{0,4},{4,8},{8,12},{1,5},{5,9},{9,13},{2,6},{6,10},{10,14},{3,7},{... | collective-permute-start | bytes 12296 | tf_op jit(solution)/shard_map/ppermute | solution.py:22
  217.2 1.3 collective-permute-start.5
  218.6 0.3 collective-permute-done.4
  218.8 4.2 %collective-permute-done.5 = bf16[4,1,32,16]{3,2,1,0:T(8,128)(2,1)S(1)} collective-permute-done((bf16[4,1,32,16]{3,2,1,0:T(8,128)(2,1)S(1)}, bf16[4,1,32,16]{3,2,1,0:T(8,128)(2,1)S(1)}, u32[]{:S(2)}, u32[]{:S(2)}) %collective-permute-start.5) | collective-permute-done | bytes 4128 | tf_op jit(solution)/shard_map/ppermute | solution.py:23
  223.3 0.3 concatenate.112
  223.7 0.4 copy-done.3
  224.1 0.3 multiply_reduce_fusion
  224.4 0.8 multiply_convert_fusion
  (60 shorter events, 1.7 us)
Async XLA Ops:
  7.2 200.8 %copy-start = (bf16[5120,64]{0,1:T(8,128)(2,1)S(1)}, bf16[5120,64]{0,1:T(8,128)(2,1)}, u32[]{:S(2)}) copy-start(bf16[5120,64]{0,1:T(8,128)(2,1)} %param.21) | copy-start | bytes 1966084
  7.2 1.0 copy-start.5
  7.2 169.0 %all-gather.2.cloned.1.call-start = ((), (), s32[]{:S(2)}) async-start(), calls=%async_computation.4 | async-start | bytes 9830400 | tf_op jit(solution)/shard_map/all_gather | solution.py:177
  18.3 6.0 %copy-start.6 = (bf16[2,1,16,3072]{3,2,1,0:T(8,128)(2,1)S(1)}, bf16[2,1,16,3072]{3,2,1,0:T(8,128)(2,1)}, u32[]{:S(2)}) copy-start(bf16[2,1,16,3072]{3,2,1,0:T(8,128)(2,1)} %param.15) | copy-start | bytes 589828
  20.6 12.7 %copy-start.7 = (bf16[2,1,16,3072]{3,2,1,0:T(8,128)(2,1)S(1)}, bf16[2,1,16,3072]{3,2,1,0:T(8,128)(2,1)}, u32[]{:S(2)}) copy-start(bf16[2,1,16,3072]{3,2,1,0:T(8,128)(2,1)} %param.13) | copy-start | bytes 589828
  20.6 23.7 %collective-permute-start = (bf16[8,1,16,768]{3,2,0,1:T(8,128)(2,1)S(1)}, bf16[8,1,16,768]{3,2,0,1:T(8,128)(2,1)}, u32[]{:S(2)}, u32[]{:S(2)}) collective-permute-start(bf16[8,1,16,768]{3,2,0,1:T(8,128)(2,1)S(1)} %bitcast.110), channel_id=1, source_target_pairs={{0,12},{4,0},{8,4},{12,8},{1,13},{5,1},{9,5},{13,9},{2,14},{6,2},{... | collective-permute-start | bytes 589832 | tf_op jit(solution)/shard_map/ppermute | solution.py:132
  28.4 9.1 %all-to-all-start.2 = ((bf16[4,2,12288]{2,1,0:T(2,128)(2,1)}), bf16[4,2,12288]{2,1,0:T(2,128)(2,1)S(1)}, u32[]{:S(2)}, u32[]{:S(2)}) async-start(bf16[4,2,12288]{2,1,0:T(2,128)(2,1)} %reshape.126), calls=%async_computation.2 | async-start | bytes 393216 | tf_op jit(solution)/shard_map/all_to_all | solution.py:153
  37.5 51.7 %all-to-all-start.1 = ((bf16[4,2,12288]{2,1,0:T(2,128)(2,1)}), bf16[4,2,12288]{2,1,0:T(2,128)(2,1)S(1)}, u32[]{:S(2)}, u32[]{:S(2)}) async-start(bf16[4,2,12288]{2,1,0:T(2,128)(2,1)} %reshape.124), calls=%async_computation.1 | async-start | bytes 393216 | tf_op jit(solution)/shard_map/all_to_all | solution.py:151
  42.0 164.3 %reduce-scatter.2.cloned.1.call-start = ((), (), s32[]{:S(2)}) async-start(), calls=%async_computation.5 | async-start | bytes 1638400 | tf_op jit(solution)/shard_map/reduce_scatter | solution.py:181
  44.3 49.4 %collective-permute-start.1 = (bf16[8,1,16,768]{3,2,0,1:T(8,128)(2,1)}, bf16[8,1,16,768]{3,2,0,1:T(8,128)(2,1)}, u32[]{:S(2)}, u32[]{:S(2)}) collective-permute-start(bf16[8,1,16,768]{3,2,0,1:T(8,128)(2,1)} %collective-permute-done), channel_id=1, source_target_pairs={{0,12},{4,0},{8,4},{12,8},{1,13},{5,1},{9,5},{13,9},{2,14},{6,2},{... | collective-permute-start | bytes 589832 | tf_op jit(solution)/shard_map/ppermute | solution.py:132
  93.8 15.7 %collective-permute-start.2 = (bf16[8,1,16,768]{3,2,0,1:T(8,128)(2,1)}, bf16[8,1,16,768]{3,2,0,1:T(8,128)(2,1)S(1)}, u32[]{:S(2)}, u32[]{:S(2)}) collective-permute-start(bf16[8,1,16,768]{3,2,0,1:T(8,128)(2,1)} %collective-permute-done.1), channel_id=1, source_target_pairs={{0,12},{4,0},{8,4},{12,8},{1,13},{5,1},{9,5},{13,9},{2,14},{6,2},{... | collective-permute-start | bytes 589832 | tf_op jit(solution)/shard_map/ppermute | solution.py:132
  112.4 1.2 copy-start.2
  114.7 67.1 %copy-start.9 = (f32[5120]{0:T(1024)S(1)}, f32[5120]{0:T(1024)}, u32[]{:S(2)}) copy-start(f32[5120]{0:T(1024)} %param.20) | copy-start | bytes 61444
  114.8 91.5 %copy-start.10 = (f32[5120]{0:T(1024)S(1)}, f32[5120]{0:T(1024)}, u32[]{:S(2)}) copy-start(f32[5120]{0:T(1024)} %param.18) | copy-start | bytes 61444
  181.8 24.5 %copy-start.4 = (bf16[2,1,16,5120]{3,2,1,0:T(8,128)(2,1)S(1)}, bf16[2,1,16,5120]{3,2,1,0:T(8,128)(2,1)}, u32[]{:S(2)}) copy-start(bf16[2,1,16,5120]{3,2,1,0:T(8,128)(2,1)} %param.16) | copy-start | bytes 983044
  181.8 26.0 %copy-start.8 = (f32[5120]{0:T(1024)S(1)}, f32[5120]{0:T(1024)}, u32[]{:S(2)}) copy-start(f32[5120]{0:T(1024)} %param.19) | copy-start | bytes 61444
  181.8 26.2 %copy-start.13 = (f32[64]{0:T(128)S(1)}, f32[64]{0:T(128)}, u32[]{:S(2)}) copy-start(f32[64]{0:T(128)} %param.22) | copy-start | bytes 772
  207.5 15.8 %copy-start.1 = (bf16[2,1,16,5120]{3,2,0,1:T(8,128)(2,1)}, bf16[2,1,16,5120]{3,2,0,1:T(8,128)(2,1)S(1)}, u32[]{:S(2)}) copy-start(bf16[2,1,16,5120]{3,2,0,1:T(8,128)(2,1)S(1)} %get-tuple-element.36) | copy-start | bytes 983044
  208.4 5.2 %collective-permute-start.3 = (bf16[2,2,32,16]{3,2,1,0:T(8,128)(2,1)S(1)}, bf16[2,2,32,16]{3,2,1,0:T(8,128)(2,1)S(1)}, u32[]{:S(2)}, u32[]{:S(2)}) collective-permute-start(bf16[2,2,32,16]{3,2,1,0:T(8,128)(2,1)S(1)} %bitcast.114), channel_id=1, source_target_pairs={{0,1},{1,2},{2,3},{4,5},{5,6},{6,7},{8,9},{9,10},{10,11},{12,13},{... | collective-permute-start | bytes 12296 | tf_op jit(solution)/shard_map/ppermute | solution.py:12
  213.6 5.2 %collective-permute-start.4 = (bf16[4,1,32,16]{3,2,1,0:T(8,128)(2,1)S(1)}, bf16[4,1,32,16]{3,2,1,0:T(8,128)(2,1)S(1)}, u32[]{:S(2)}, u32[]{:S(2)}) collective-permute-start(bf16[4,1,32,16]{3,2,1,0:T(8,128)(2,1)S(1)} %get-tuple-element.63), channel_id=1, source_target_pairs={{0,4},{4,8},{8,12},{1,5},{5,9},{9,13},{2,6},{6,10},{10,14},{3,7},{... | collective-permute-start | bytes 12296 | tf_op jit(solution)/shard_map/ppermute | solution.py:22
  217.2 5.8 %collective-permute-start.5 = (bf16[4,1,32,16]{3,2,1,0:T(8,128)(2,1)S(1)}, bf16[4,1,32,16]{3,2,1,0:T(8,128)(2,1)S(1)}, u32[]{:S(2)}, u32[]{:S(2)}) collective-permute-start(bf16[4,1,32,16]{3,2,1,0:T(8,128)(2,1)S(1)} %get-tuple-element.64), channel_id=1, source_target_pairs={{4,0},{8,4},{12,8},{5,1},{9,5},{13,9},{6,2},{10,6},{14,10},{7,3},{... | collective-permute-start | bytes 12296 | tf_op jit(solution)/shard_map/ppermute | solution.py:23
  223.1 1.0 copy-start.3
  223.1 1.0 copy-start.11
  223.1 1.3 copy-start.12
Sparse Core Ops, SparseCore 0:
  9.6 166.5 all-gather.1
  181.9 24.3 reduce-scatter.1
